TPU v7x, 32 devices: a whole 2x2x4 slice. The times are simulated.
32 devices in a mesh: kpt: 2 (over x), row: 8 (over z, y), col: 2 (over core).
Axes of the slice: x: 2, y: 2, z: 4, core: 2. Of those that a mesh axis runs over, the one named last changes fastest.
Arguments:
- wannier: float32 [64, 32, 1024], P('kpt', ('row', 'col')), parts along dimension 0, may hold values from -6 to 6
- pairs: int32 [384, 2], replicated, may hold values from 0 to 31, as said below
- gmap: int32 [8192], replicated, may hold values from 1 to 32767, as said below
- screened: bfloat16 [4, 2, 8192, 8192], P('kpt', None, 'row', 'col'), parts along dimension 0, may hold values from -0.046875 to 0.046875
Outputs:
- coulomb: float32 [2, 2, 768, 384], P(None, None, ('kpt', 'row', 'col')), parts along dimension 2
There are 2 independent parts, one for each index of `kpt`. A program takes and returns all parts, laid end to end along the dimension named above; an argument that names none is the same for every part. Nothing has to cross between parts.
Inputs may be any that keep to these rules, and one draw needn't show every extreme that they name: `gmap`: 8192 distinct flat cells of the grid; cell 0 is never among them. `pairs`: in each row the first Wannier function is no greater than the second; no two rows are equal.
All inputs are finite; a program needn't handle non-finite values.
Results may differ from a plain program's by a relative error of at most 0.0082.
Values may be sent and summed in bfloat16 or wider, within the bound.
No kernel may reach another device: no remote copies, remote signals or barrier semaphores. Data moves between devices by JAX's collectives and lax.ppermute only.
A program may use at most 128 MiB of HBM per device.

v0:
```python
import math
import jax
import jax.numpy as jnp
from jax import lax
from jax.sharding import PartitionSpec as P

NW = 32
GX = 32
NG = 8192
NP = 384


def line_tables(side_len):
    positions = jnp.arange(side_len, dtype=jnp.int32)
    phase_index = positions[:, None] * positions[None, :] % side_len
    angles = phase_index.astype(jnp.float32) * (2.0 * math.pi / side_len)
    return (jnp.cos(angles), jnp.sin(angles))


def plane_transform(density):
    cosine, sine_table = line_tables(GX)
    highest = lax.Precision.HIGHEST
    shaped = density.reshape(-1, GX, GX)
    real_z = jnp.einsum("nyz,kz->nyk", shaped, cosine, precision=highest)
    imag_z = -jnp.einsum("nyz,kz->nyk", shaped, sine_table, precision=highest)
    new_real = jnp.einsum("jy,nyk->njk", cosine, real_z, precision=highest) + jnp.einsum(
        "jy,nyk->njk", sine_table, imag_z, precision=highest
    )
    new_imag = jnp.einsum("jy,nyk->njk", cosine, imag_z, precision=highest) - jnp.einsum(
        "jy,nyk->njk", sine_table, real_z, precision=highest
    )
    return (new_real.reshape(density.shape), new_imag.reshape(density.shape))


def line_transform(real_part, imag_part):
    cosine, sine_table = line_tables(GX)
    highest = lax.Precision.HIGHEST
    new_real = jnp.einsum("kn,pny->pky", cosine, real_part, precision=highest) + jnp.einsum(
        "kn,pny->pky", sine_table, imag_part, precision=highest
    )
    new_imag = jnp.einsum("kn,pny->pky", cosine, imag_part, precision=highest) - jnp.einsum(
        "kn,pny->pky", sine_table, real_part, precision=highest
    )
    return (new_real, new_imag)


def right_columns(screened, segment):
    w_real = screened[:, 0]
    w_imag = screened[:, 1]
    real_real = jnp.einsum("fgh,bh->fgb", w_real, segment[0], preferred_element_type=jnp.float32)
    imag_imag = jnp.einsum("fgh,bh->fgb", w_imag, segment[1], preferred_element_type=jnp.float32)
    real_imag = jnp.einsum("fgh,bh->fgb", w_real, segment[1], preferred_element_type=jnp.float32)
    imag_real = jnp.einsum("fgh,bh->fgb", w_imag, segment[0], preferred_element_type=jnp.float32)
    return jnp.stack([real_real - imag_imag, real_imag + imag_real], axis=1)


def shards(wannier, pairs, gmap, screened):
    planes = wannier.shape[1]
    grid_cells = wannier.shape[2]
    members = jnp.arange(NW, dtype=jnp.int32)[None, :]
    pick_first = (pairs[:, 0:1] == members).astype(jnp.float32)
    pick_second = (pairs[:, 1:2] == members).astype(jnp.float32)
    flat_rows = wannier.reshape(NW, -1)
    highest = lax.Precision.HIGHEST
    density = jnp.dot(pick_first, flat_rows, precision=highest) * jnp.dot(
        pick_second, flat_rows, precision=highest
    )
    density = density.reshape(NP, planes, grid_cells)
    arrived = lax.all_to_all(density, ("row", "col"), split_axis=0, concat_axis=1, tiled=True)
    real_part, imag_part = plane_transform(arrived)
    real_part, imag_part = line_transform(real_part, imag_part)
    owned = real_part.shape[0]
    norm_factor = 1.0 / math.sqrt(GX * GX * GX)
    rho_real = jnp.take(real_part.reshape(owned, -1), gmap, axis=1) * norm_factor
    rho_imag = jnp.take(imag_part.reshape(owned, -1), gmap, axis=1) * norm_factor
    rho = jnp.stack([rho_real, rho_imag], axis=0).astype(jnp.bfloat16)
    row_span = screened.shape[2]
    halves = lax.all_to_all(rho, "col", split_axis=2, concat_axis=1, tiled=True)
    screened_rho = right_columns(screened, lax.all_gather(halves, "row", axis=1, tiled=True))
    blocks = lax.all_to_all(rho, "row", split_axis=2, concat_axis=1, tiled=True)
    blocks = blocks.reshape(2, lax.axis_size("row"), owned, row_span)
    left_panel = lax.all_gather(blocks, "col", axis=2, tiled=True).reshape(2, NP, row_span)
    left_wide = left_panel.astype(jnp.float32)
    u_real = jnp.einsum(
        "ag,fgb->fab", left_wide[0], screened_rho[:, 0], precision=highest
    ) + jnp.einsum("ag,fgb->fab", left_wide[1], screened_rho[:, 1], precision=highest)
    u_imag = jnp.einsum(
        "ag,fgb->fab", left_wide[0], screened_rho[:, 1], precision=highest
    ) - jnp.einsum("ag,fgb->fab", left_wide[1], screened_rho[:, 0], precision=highest)
    partial_terms = jnp.stack([u_real, u_imag], axis=1) / math.sqrt(NG)
    summed = lax.psum(partial_terms, ("row", "col"))
    share_rows = NP // lax.axis_size(("row", "col"))
    return lax.dynamic_slice_in_dim(
        summed, lax.axis_index(("row", "col")) * share_rows, share_rows, 2
    )


def solution(mesh):
    return jax.shard_map(
        shards,
        mesh=mesh,
        in_specs=(P("kpt", ("row", "col"), None), P(), P(), P("kpt", None, "row", "col")),
        out_specs=P(None, None, ("kpt", "row", "col"), None),
        check_vma=False,
    )
```

profile of v0, /device:TPU:0, one launch (start us, length us, event | category | flops | bytes accessed | tf_op | source)
XLA Modules:
  0.0 687.3 jit_solution(8600309741713015094)
XLA Ops:
  6.5 0.8 slice_reduce_fusion
  7.3 1.0 copy.93
  8.3 1.4 fusion.54
  9.8 1.5 convolution_multiply_fusion
  11.3 3.8 reshape.35
  15.1 7.5 %all-to-all-start = ((f32[384,2,1024]{2,1,0:T(2,128)}), f32[384,2,1024]{2,1,0:T(2,128)S(1)}, u32[]{:S(2)}, u32[]{:S(2)}) async-start(f32[384,2,1024]{2,1,0:T(2,128)} %reshape.35), calls=%async_computation | async-start | bytes 6291456 | tf_op jit(solution)/shard_map/all_to_all | solution.py:69
  22.6 0.0 all-gather.5.cloned.1.call-start
  22.7 0.0 copy-done.4
  22.7 59.1 %all-to-all-done = f32[384,2,1024]{2,1,0:T(2,128)S(1)} async-done(((f32[384,2,1024]{2,1,0:T(2,128)}), f32[384,2,1024]{2,1,0:T(2,128)S(1)}, u32[]{:S(2)}, u32[]{:S(2)}) %all-to-all-start) | async-done | bytes 3145760 | tf_op jit(solution)/shard_map/all_to_all | solution.py:69
  81.9 1.0 copy.70
  82.9 2.4 copy.71
  85.3 7.6 %reshape.36 = f32[768,32,32]{2,1,0:T(8,128)} reshape(f32[24,16,2,1024]{3,2,1,0:T(2,128)S(1)} %copy.71) | data formatting | bytes 6291456 | tf_op jit(solution)/shard_map/reshape | solution.py:23
  92.9 9.2 %copy.72 = f32[768,32,32]{0,2,1:T(8,128)S(1)} copy(f32[768,32,32]{2,1,0:T(8,128)} %reshape.36) | data formatting | bytes 6291456 | tf_op jit(solution)/shard_map/reshape | solution.py:23
  102.1 3.0 convolution_negate_fusion
  105.1 3.0 fusion.72
  108.1 4.9 fusion.22
  113.1 5.2 fusion.24
  118.2 6.7 add_bitcast_fusion.1
  125.0 5.5 subtract_bitcast_fusion.1
  130.5 10.6 %copy.79 = f32[768,32,32]{2,1,0:T(8,128)} copy(f32[768,32,32]{0,1,2:T(8,128)S(1)} %subtract_bitcast_fusion.1) | data formatting | bytes 6291456 | tf_op jit(solution)/shard_map/sub | solution.py:29
  141.1 9.4 %reshape.38 = f32[24,32,1024]{2,1,0:T(8,128)S(1)} reshape(f32[768,32,32]{2,1,0:T(8,128)} %copy.79) | data formatting | bytes 6291456 | tf_op jit(solution)/shard_map/reshape | solution.py:32
  150.4 5.5 fusion.66
  155.9 11.4 %copy.76 = f32[768,32,32]{2,1,0:T(8,128)} copy(f32[768,32,32]{0,1,2:T(8,128)} %add_bitcast_fusion.1) | data formatting | bytes 6291456 | tf_op jit(solution)/shard_map/add | solution.py:26
  167.3 10.7 %reshape.37 = f32[24,32,1024]{2,1,0:T(8,128)} reshape(f32[768,32,32]{2,1,0:T(8,128)} %copy.76) | data formatting | bytes 6291456 | tf_op jit(solution)/shard_map/reshape | solution.py:32
  178.0 5.9 fusion.69
  184.0 5.5 subtract_bitcast_fusion
  189.5 5.6 add_bitcast_fusion
  195.1 10.3 %copy.89 = f32[24,32,1024]{0,2,1:T(8,128)} copy(f32[24,32,1024]{2,1,0:T(8,128)} %add_bitcast_fusion) | data formatting | bytes 6291456 | tf_op jit(solution)/shard_map/reshape | solution.py:74
  205.4 0.0 copy-done.2
  205.4 8.6 %copy.90 = f32[24,32,1024]{0,2,1:T(8,128)} copy(f32[24,32,1024]{2,1,0:T(8,128)S(1)} %copy-done.2) | data formatting | bytes 6291456 | tf_op jit(solution)/shard_map/reshape | solution.py:75
  214.0 33.6 %gather_fusion = f32[8192,24]{1,0:T(8,128)} fusion(f32[24,32768]{0,1:T(8,128)} %bitcast.144, s32[8192]{0:T(1024)S(1)} %fusion.57), kind=kCustom, calls=%fused_computation.clone | custom fusion | bytes 1605632 | tf_op jit(solution)/shard_map/jit(_take)/gather | solution.py:74
  247.6 33.6 %gather_fusion.1 = f32[8192,24]{1,0:T(8,128)} fusion(f32[24,32768]{0,1:T(8,128)} %bitcast.143, s32[8192]{0:T(1024)S(1)} %fusion.57), kind=kCustom, calls=%fused_computation.1.clone | custom fusion | bytes 1605632 | tf_op jit(solution)/shard_map/jit(_take)/gather | solution.py:75
  281.3 7.2 %fusion.30 = (bf16[1,24,8192]{1,2,0:T(8,128)(2,1)S(1)}, bf16[1,24,8192]{1,2,0:T(8,128)(2,1)S(1)}) fusion(f32[8192,24]{1,0:T(8,128)} %gather_fusion, pred[8192]{0:T(1024)(128)(4,1)S(1)} %compare_and_fusion, f32[8192,24]{1,0:T(8,128)} %gather_fusion.1), kind=kLoop, calls=%fused_computation.43 | loop fusion | flops 1179648 | bytes 2367488 | tf_op jit(solution)/shard_map/stack | solution.py:76
  288.4 0.9 pad_maximum_fusion
  289.4 35.5 %copy.108 = bf16[2,24,8192]{1,0,2:T(2,128)(2,1)} copy(bf16[2,24,8192]{1,2,0:T(8,128)(2,1)S(1)} %pad_maximum_fusion) | data formatting | bytes 1572864 | tf_op jit(solution)/shard_map/stack | solution.py:76
  324.9 6.6 reshape.71
  331.5 35.8 %all_to_all.48 = bf16[8,2,24576]{2,1,0:T(2,128)(2,1)S(1)} all-to-all(bf16[8,2,24576]{2,1,0:T(2,128)(2,1)S(1)} %reshape.71), channel_id=1, replica_groups=mesh['kpt'=2,'row'=8,'col'=2] {'row'}, dimensions={0} | all-to-all | bytes 1572864 | tf_op jit(solution)/shard_map/all_to_all | solution.py:80
  367.3 6.9 %reshape.72 = bf16[8192,2,24]{2,1,0:T(2,128)(2,1)} reshape(bf16[8,2,24576]{2,1,0:T(2,128)(2,1)S(1)} %all_to_all.48) | data formatting | bytes 1572864
  374.3 10.3 %copy.87 = bf16[2,24,8,1024]{3,1,2,0:T(8,128)(2,1)} copy(bf16[2,24,8,1024]{1,0,3,2:T(2,128)(2,1)} %bitcast.145) | data formatting | bytes 1572864 | tf_op jit(solution)/shard_map/all_to_all | solution.py:80
  384.6 0.0 all-gather.5.cloned.1.call-update
  384.6 0.0 all-gather.3.cloned.1.call-start
  384.6 10.2 %copy.109 = bf16[2,24,8192]{1,0,2:T(2,128)(2,1)} copy(bf16[2,24,8192]{1,2,0:T(8,128)(2,1)} %copy-done) | data formatting | bytes 1572864 | tf_op jit(solution)/shard_map/stack | solution.py:76
  394.8 7.0 %reshape.73 = bf16[2,2,98304]{2,1,0:T(2,128)(2,1)S(1)} reshape(bf16[8192,2,24]{2,1,0:T(2,128)(2,1)} %bitcast.147) | data formatting | bytes 1572864
  401.9 4.4 all_to_all.49
  406.2 7.3 %reshape.74 = bf16[8192,2,24]{2,1,0:T(2,128)(2,1)} reshape(bf16[2,2,98304]{2,1,0:T(2,128)(2,1)S(1)} %all_to_all.49) | data formatting | bytes 1572864
  413.6 9.5 %copy.83 = bf16[2,24,2,4096]{3,1,2,0:T(8,128)(2,1)} copy(bf16[2,24,2,4096]{1,0,3,2:T(2,128)(2,1)} %bitcast.146) | data formatting | bytes 1572864 | tf_op jit(solution)/shard_map/all_to_all | solution.py:78
  423.0 0.0 all-gather.3.cloned.1.call-update
  423.1 0.0 all-reduce.2.cloned.1.call-start
  423.1 0.0 all-gather.5.cloned.1.call-done
  423.1 1.5 fusion.129
  424.7 96.3 %all-gather.3.cloned.1.call-done = bf16[2,384,4096]{2,1,0:T(8,128)(2,1)} async-done(((bf16[2,48,4096]{2,1,0:T(8,128)(2,1)}), bf16[2,384,4096]{2,1,0:T(8,128)(2,1)}) %all-gather.3.cloned.1.call-update) | async-done | bytes 6291472 | tf_op jit(solution)/shard_map/all_gather | solution.py:79
  521.0 11.4 %fusion = f32[384,2,1024]{2,0,1:T(8,128)S(1)} fusion(bf16[2,2,1024,4096]{3,2,1,0:T(8,128)(2,1)} %param.9, bf16[2,384,4096]{2,1,0:T(8,128)(2,1)} %all-gather.3.cloned.1.call-done), kind=kOutput, calls=%fused_computation.2 | convolution fusion | flops 6442450944 | bytes 23068672 | tf_op jit(solution)/shard_map/fgh,bh->fgb/dot_general | solution.py:53
  532.4 11.2 %fusion.39 = f32[384,2,1024]{2,0,1:T(8,128)S(1)} fusion(f32[384,2,1024]{2,0,1:T(8,128)S(1)} %fusion, bf16[2,2,1024,4096]{3,2,1,0:T(8,128)(2,1)} %param.9, bf16[2,384,4096]{2,1,0:T(8,128)(2,1)} %all-gather.3.cloned.1.call-done), kind=kOutput, calls=%fused_computation.47 | convolution fusion | flops 6443237376 | bytes 26214400 | tf_op jit(solution)/shard_map/fgh,bh->fgb/dot_general | solution.py:52
  543.6 2.6 fusion.14
  546.2 2.6 fusion.16
  548.9 12.6 %fusion.2 = f32[384,2,1024]{2,0,1:T(8,128)} fusion(bf16[2,2,1024,4096]{3,2,1,0:T(8,128)(2,1)} %param.9, bf16[2,384,4096]{2,1,0:T(8,128)(2,1)} %all-gather.3.cloned.1.call-done), kind=kOutput, calls=%fused_computation.4 | convolution fusion | flops 6442450944 | bytes 23068672 | tf_op jit(solution)/shard_map/fgh,bh->fgb/dot_general | solution.py:51
  561.5 12.1 %fusion.36 = f32[384,2,1024]{2,0,1:T(8,128)S(1)} fusion(f32[384,2,1024]{2,0,1:T(8,128)} %fusion.2, bf16[2,2,1024,4096]{3,2,1,0:T(8,128)(2,1)} %param.9, bf16[2,384,4096]{2,1,0:T(8,128)(2,1)} %all-gather.3.cloned.1.call-done), kind=kOutput, calls=%fused_computation.46 | convolution fusion | flops 6443237376 | bytes 26214400 | tf_op jit(solution)/shard_map/fgh,bh->fgb/dot_general | solution.py:50
  573.6 2.7 fusion.48
  576.3 2.7 fusion.51
  579.0 1.6 maximum_multiply_fusion
  580.6 0.0 all-reduce.2.cloned.1.call-update
  580.6 97.4 %all-reduce.2.cloned.1.call-done = f32[2,2,384,384]{2,3,0,1:T(8,128)} async-done(((f32[2,2,384,384]{2,3,0,1:T(8,128)}), f32[2,2,384,384]{2,3,0,1:T(8,128)}) %all-reduce.2.cloned.1.call-update) | async-done | bytes 2359312 | tf_op jit(solution)/shard_map/psum | solution.py:91
  678.0 1.7 constant_dynamic-slice_fusion
  679.6 0.9 copy.88
  (10 shorter events, 0.0 us)
Async XLA Ops:
  15.1 7.6 %copy-start.4 = (s32[8192]{0:T(1024)S(1)}, s32[8192]{0:T(1024)}, u32[]{:S(2)}) copy-start(s32[8192]{0:T(1024)} %param.8) | copy-start | bytes 98308
  15.1 66.8 %all-to-all-start = ((f32[384,2,1024]{2,1,0:T(2,128)}), f32[384,2,1024]{2,1,0:T(2,128)S(1)}, u32[]{:S(2)}, u32[]{:S(2)}) async-start(f32[384,2,1024]{2,1,0:T(2,128)} %reshape.35), calls=%async_computation | async-start | bytes 6291456 | tf_op jit(solution)/shard_map/all_to_all | solution.py:69
  22.6 400.5 %all-gather.5.cloned.1.call-start = ((), (), s32[]{:S(2)}) async-start(), calls=%async_computation.4 | async-start | bytes 2359296 | tf_op jit(solution)/shard_map/all_gather | solution.py:82
  178.0 6.0 copy-start.1
  178.0 6.0 copy-start.3
  195.1 10.3 %copy-start.2 = (f32[24,32,1024]{2,1,0:T(8,128)S(1)}, f32[24,32,1024]{2,1,0:T(8,128)}, u32[]{:S(2)}) copy-start(f32[24,32,1024]{2,1,0:T(8,128)} %subtract_bitcast_fusion) | copy-start | bytes 9437188
  289.4 35.5 %copy-start = (bf16[2,24,8192]{1,2,0:T(8,128)(2,1)}, bf16[2,24,8192]{1,2,0:T(8,128)(2,1)S(1)}, u32[]{:S(2)}) copy-start(bf16[2,24,8192]{1,2,0:T(8,128)(2,1)S(1)} %pad_maximum_fusion) | copy-start | bytes 2359300
  384.6 136.4 %all-gather.3.cloned.1.call-start = ((), (), s32[]{:S(2)}) async-start(), calls=%async_computation.3 | async-start | bytes 7077888 | tf_op jit(solution)/shard_map/all_gather | solution.py:79
  423.1 254.9 %all-reduce.2.cloned.1.call-start = ((), (), s32[]{:S(2)}) async-start(), calls=%async_computation.5 | async-start | bytes 4718592 | tf_op jit(solution)/shard_map/psum | solution.py:91
Sparse Core Ops, SparseCore 0:
  384.7 8.8 all-gather.4
  423.2 97.7 all-gather.2
  580.7 97.1 all-reduce.1
where the time goes:
time: 696 us; the launch traced here: 687 us
  waiting for transfers between devices  253 us (36%)
  local copies, waits for them, and re-layouts  251 us (36%)
  matrix products  112 us (16%)
  blocking collectives  40.2 us (6%)
  between operations  13.7 us (2%)
  other arithmetic  9.75 us (1%)
  starting transfers between devices  7.67 us (1%)
    psum x1, waiting for transfers between devices, shards(): summed = lax.psum(partial_terms, ('row', 'col'))  97.4 us
    all_gather x1, waiting for transfers between devices, shards(): lax.all_gather(halves, 'row', axis=1, tiled=True)  96.3 us
    all_to_all x1, waiting for transfers between devices, shards(): lax.all_to_all(density, ('row', 'col'), split_axis=0, concat_axis=1, tile...  59.1 us
    another operation x2, local copies, waits for them, and re-layouts, shards(): rho = jnp.stack([rho_real, rho_imag], axis=0).astype(jnp.bfloat16)  45.7 us
    all_to_all x1, blocking collectives, shards(): blocks = lax.all_to_all(rho, 'row', split_axis=2, concat_axis=1, tiled=True)  35.8 us
    gather x1, local copies, waits for them, and re-layouts, shards(): jnp.take(imag_part.reshape(owned, -1), gmap, axis=1) * norm_factor  33.6 us
    gather x1, local copies, waits for them, and re-layouts, shards(): jnp.take(real_part.reshape(owned, -1), gmap, axis=1) * norm_factor  33.6 us
    unnamed x15, local copies, waits for them, and re-layouts  29 us
  transfers between devices with their start and end apart: 4, of which 3 were waited for; matrix products, arithmetic and copies ran while one was open for 5% of the time, Pallas kernels for 0%

commit v1 on v0

--- a/solution.py
+++ b/solution.py
@@ -88,7 +88,7 @@
         "ag,fgb->fab", left_wide[0], screened_rho[:, 1], precision=highest
     ) - jnp.einsum("ag,fgb->fab", left_wide[1], screened_rho[:, 0], precision=highest)
     partial_terms = jnp.stack([u_real, u_imag], axis=1) / math.sqrt(NG)
-    summed = lax.psum(partial_terms, ("row", "col"))
+    summed = jnp.sum(lax.all_gather(partial_terms, ("row", "col")), axis=0)
     share_rows = NP // lax.axis_size(("row", "col"))
     return lax.dynamic_slice_in_dim(
         summed, lax.axis_index(("row", "col")) * share_rows, share_rows, 2

time: 696 us -> 807 us (1.16)
  waiting for transfers between devices: 253 us -> 342 us
  other arithmetic: 9.75 us -> 21.4 us
    all_gather x0 -> x1, waiting for transfers between devices: none -> 186 us  [shards(): summed = jnp.sum(lax.all_gather(partial_terms, ('row', 'col')), axis=0)]
    psum x1 -> x0, waiting for transfers between devices: 97.4 us -> none  [shards(): summed = lax.psum(partial_terms, ('row', 'col'))]
    reduce_sum x0 -> x1, other arithmetic: none -> 13.5 us  [shards(): summed = jnp.sum(lax.all_gather(partial_terms, ('row', 'col')), axis=0)]
    unnamed x15 -> x17, local copies, waits for them, and re-layouts: 29 us -> 30.6 us
  transfers between devices with their start and end apart: 4 -> 4, of which waited for: 3 -> 3; matrix products, arithmetic and copies ran while one was open for 5% -> 4% of each run, Pallas kernels for 0% -> 0%
where the time goes in v1:
time: 807 us; the launch traced here: 798 us
  waiting for transfers between devices  342 us (42%)
  local copies, waits for them, and re-layouts  256 us (32%)
  matrix products  118 us (15%)
  blocking collectives  40.2 us (5%)
  other arithmetic  21.4 us (3%)
  between operations  13.6 us (2%)
    all_gather x1, waiting for transfers between devices, shards(): summed = jnp.sum(lax.all_gather(partial_terms, ('row', 'col')), axis=0)  186 us
    all_gather x1, waiting for transfers between devices, shards(): lax.all_gather(halves, 'row', axis=1, tiled=True)  96.3 us
    all_to_all x1, waiting for transfers between devices, shards(): lax.all_to_all(density, ('row', 'col'), split_axis=0, concat_axis=1, tile...  59.1 us
    another operation x2, local copies, waits for them, and re-layouts, shards(): rho = jnp.stack([rho_real, rho_imag], axis=0).astype(jnp.bfloat16)  46.1 us
    all_to_all x1, blocking collectives, shards(): blocks = lax.all_to_all(rho, 'row', split_axis=2, concat_axis=1, tiled=True)  35.8 us
    gather x1, local copies, waits for them, and re-layouts, shards(): jnp.take(imag_part.reshape(owned, -1), gmap, axis=1) * norm_factor  33.5 us
    gather x1, local copies, waits for them, and re-layouts, shards(): jnp.take(real_part.reshape(owned, -1), gmap, axis=1) * norm_factor  33.5 us
    unnamed x17, local copies, waits for them, and re-layouts  30.6 us
  transfers between devices with their start and end apart: 4, of which 3 were waited for; matrix products, arithmetic and copies ran while one was open for 4% of the time, Pallas kernels for 0%

profile of v1, /device:TPU:0, one launch (start us, length us, event | category | flops | bytes accessed | tf_op | source)
XLA Modules:
  0.0 798.1 jit_solution(6940244225572223002)
XLA Ops:
  6.5 1.0 copy.96
  7.6 0.8 slice_reduce_fusion
  8.3 1.4 fusion.54
  9.8 1.5 convolution_multiply_fusion
  11.3 3.8 reshape.66
  15.1 7.5 all-to-all-start
  22.6 0.0 all-gather.6.cloned.1.call-start
  22.7 59.1 %all-to-all-done = f32[384,2,1024]{2,1,0:T(2,128)S(1)} async-done(((f32[384,2,1024]{2,1,0:T(2,128)}), f32[384,2,1024]{2,1,0:T(2,128)S(1)}, u32[]{:S(2)}, u32[]{:S(2)}) %all-to-all-start) | async-done | bytes 3145760 | tf_op jit(solution)/shard_map/all_to_all | solution.py:69
  81.8 1.0 copy.69
  82.9 2.4 copy.70
  85.3 7.5 reshape.67
  92.8 9.2 %copy.71 = f32[768,32,32]{0,2,1:T(8,128)S(1)} copy(f32[768,32,32]{2,1,0:T(8,128)} %reshape.67) | data formatting | bytes 6291456 | tf_op jit(solution)/shard_map/reshape | solution.py:23
  102.1 1.6 copy-done.1
  103.7 3.0 convolution_negate_fusion
  106.7 4.8 fusion.72
  111.5 4.9 fusion.22
  116.4 6.7 fusion.24
  123.1 6.7 subtract_bitcast_fusion.1
  129.8 11.4 %copy.78 = f32[768,32,32]{2,1,0:T(8,128)} copy(f32[768,32,32]{0,1,2:T(8,128)} %subtract_bitcast_fusion.1) | data formatting | bytes 6291456 | tf_op jit(solution)/shard_map/sub | solution.py:29
  141.2 10.9 %reshape.69 = f32[24,32,1024]{2,1,0:T(8,128)} reshape(f32[768,32,32]{2,1,0:T(8,128)} %copy.78) | data formatting | bytes 6291456 | tf_op jit(solution)/shard_map/reshape | solution.py:32
  152.1 7.5 fusion.66
  159.7 6.7 add_bitcast_fusion.1
  166.4 11.4 %copy.75 = f32[768,32,32]{2,1,0:T(8,128)} copy(f32[768,32,32]{0,1,2:T(8,128)} %add_bitcast_fusion.1) | data formatting | bytes 6291456 | tf_op jit(solution)/shard_map/add | solution.py:26
  177.8 9.5 %reshape.68 = f32[24,32,1024]{2,1,0:T(8,128)S(1)} reshape(f32[768,32,32]{2,1,0:T(8,128)} %copy.75) | data formatting | bytes 6291456 | tf_op jit(solution)/shard_map/reshape | solution.py:32
  187.3 5.5 fusion.69
  192.8 5.6 subtract_bitcast_fusion
  198.4 10.2 %copy.91 = f32[24,32,1024]{0,2,1:T(8,128)} copy(f32[24,32,1024]{2,1,0:T(8,128)} %subtract_bitcast_fusion) | data formatting | bytes 6291456 | tf_op jit(solution)/shard_map/reshape | solution.py:75
  208.6 6.0 add_bitcast_fusion
  214.6 10.1 %copy.90 = f32[24,32,1024]{0,2,1:T(8,128)} copy(f32[24,32,1024]{2,1,0:T(8,128)} %add_bitcast_fusion) | data formatting | bytes 6291456 | tf_op jit(solution)/shard_map/reshape | solution.py:74
  224.7 33.5 %gather_fusion.1 = f32[8192,24]{1,0:T(8,128)} fusion(f32[24,32768]{0,1:T(8,128)} %bitcast.143, s32[8192]{0:T(1024)S(1)} %fusion.57), kind=kCustom, calls=%fused_computation.1.clone | custom fusion | bytes 1605632 | tf_op jit(solution)/shard_map/jit(_take)/gather | solution.py:75
  258.2 33.5 %gather_fusion = f32[8192,24]{1,0:T(8,128)} fusion(f32[24,32768]{0,1:T(8,128)} %bitcast.144, s32[8192]{0:T(1024)S(1)} %fusion.57), kind=kCustom, calls=%fused_computation.clone | custom fusion | bytes 1605632 | tf_op jit(solution)/shard_map/jit(_take)/gather | solution.py:74
  291.7 6.8 fusion.30
  298.4 0.9 pad_maximum_fusion
  299.4 35.9 %copy.111 = bf16[2,24,8192]{1,0,2:T(2,128)(2,1)} copy(bf16[2,24,8192]{1,2,0:T(8,128)(2,1)S(1)} %pad_maximum_fusion) | data formatting | bytes 1572864 | tf_op jit(solution)/shard_map/stack | solution.py:76
  335.3 6.6 reshape.102
  341.9 35.8 %all_to_all.48 = bf16[8,2,24576]{2,1,0:T(2,128)(2,1)S(1)} all-to-all(bf16[8,2,24576]{2,1,0:T(2,128)(2,1)S(1)} %reshape.102), channel_id=1, replica_groups=mesh['kpt'=2,'row'=8,'col'=2] {'row'}, dimensions={0} | all-to-all | bytes 1572864 | tf_op jit(solution)/shard_map/all_to_all | solution.py:80
  377.7 6.9 reshape.103
  384.6 10.3 %copy.86 = bf16[2,24,8,1024]{3,1,2,0:T(8,128)(2,1)} copy(bf16[2,24,8,1024]{1,0,3,2:T(2,128)(2,1)} %bitcast.145) | data formatting | bytes 1572864 | tf_op jit(solution)/shard_map/all_to_all | solution.py:80
  394.9 0.0 all-gather.6.cloned.1.call-update
  395.0 0.0 all-gather.4.cloned.1.call-start
  395.0 10.2 %copy.112 = bf16[2,24,8192]{1,0,2:T(2,128)(2,1)} copy(bf16[2,24,8192]{1,2,0:T(8,128)(2,1)} %copy-done) | data formatting | bytes 1572864 | tf_op jit(solution)/shard_map/stack | solution.py:76
  405.2 7.0 reshape.104
  412.2 4.4 all_to_all.49
  416.6 7.3 reshape.105
  423.9 9.4 %copy.82 = bf16[2,24,2,4096]{3,1,2,0:T(8,128)(2,1)} copy(bf16[2,24,2,4096]{1,0,3,2:T(2,128)(2,1)} %bitcast.146) | data formatting | bytes 1572864 | tf_op jit(solution)/shard_map/all_to_all | solution.py:78
  433.4 0.0 all-gather.4.cloned.1.call-update
  433.4 0.0 all-gather.8.cloned.1.call-start
  433.4 0.0 all-gather.6.cloned.1.call-done
  433.5 1.5 fusion.129
  435.0 96.3 %all-gather.4.cloned.1.call-done = bf16[2,384,4096]{2,1,0:T(8,128)(2,1)} async-done(((bf16[2,48,4096]{2,1,0:T(8,128)(2,1)}), bf16[2,384,4096]{2,1,0:T(8,128)(2,1)}) %all-gather.4.cloned.1.call-update) | async-done | bytes 6291472 | tf_op jit(solution)/shard_map/all_gather | solution.py:79
  531.3 11.4 %fusion = f32[384,2,1024]{2,0,1:T(8,128)S(1)} fusion(bf16[2,2,1024,4096]{3,2,1,0:T(8,128)(2,1)} %param.9, bf16[2,384,4096]{2,1,0:T(8,128)(2,1)} %all-gather.4.cloned.1.call-done), kind=kOutput, calls=%fused_computation.2 | convolution fusion | flops 6442450944 | bytes 23068672 | tf_op jit(solution)/shard_map/fgh,bh->fgb/dot_general | solution.py:53
  542.7 11.2 %fusion.39 = f32[384,2,1024]{2,0,1:T(8,128)S(1)} fusion(f32[384,2,1024]{2,0,1:T(8,128)S(1)} %fusion, bf16[2,2,1024,4096]{3,2,1,0:T(8,128)(2,1)} %param.9, bf16[2,384,4096]{2,1,0:T(8,128)(2,1)} %all-gather.4.cloned.1.call-done), kind=kOutput, calls=%fused_computation.47 | convolution fusion | flops 6443237376 | bytes 26214400 | tf_op jit(solution)/shard_map/fgh,bh->fgb/dot_general | solution.py:52
  553.9 2.6 fusion.16
  556.5 2.6 fusion.14
  559.2 12.6 %fusion.2 = f32[384,2,1024]{2,0,1:T(8,128)} fusion(bf16[2,2,1024,4096]{3,2,1,0:T(8,128)(2,1)} %param.9, bf16[2,384,4096]{2,1,0:T(8,128)(2,1)} %all-gather.4.cloned.1.call-done), kind=kOutput, calls=%fused_computation.4 | convolution fusion | flops 6442450944 | bytes 23068672 | tf_op jit(solution)/shard_map/fgh,bh->fgb/dot_general | solution.py:51
  571.8 11.8 %fusion.36 = f32[384,2,1024]{2,0,1:T(8,128)S(1)} fusion(f32[384,2,1024]{2,0,1:T(8,128)} %fusion.2, bf16[2,2,1024,4096]{3,2,1,0:T(8,128)(2,1)} %param.9, bf16[2,384,4096]{2,1,0:T(8,128)(2,1)} %all-gather.4.cloned.1.call-done), kind=kOutput, calls=%fused_computation.46 | convolution fusion | flops 6443237376 | bytes 26214400 | tf_op jit(solution)/shard_map/fgh,bh->fgb/dot_general | solution.py:50
  583.6 2.7 fusion.51
  586.3 2.6 fusion.48
  588.9 0.2 maximum_multiply_fusion
  589.1 1.9 copy.87
  591.1 0.0 all-gather.8.cloned.1.call-update
  591.1 186.1 %all-gather.8.cloned.1.call-done = f32[16,2,2,384,384]{4,3,2,1,0:T(8,128)} async-done(((f32[1,2,2,384,384]{4,3,2,1,0:T(8,128)}), f32[16,2,2,384,384]{4,3,2,1,0:T(8,128)}) %all-gather.8.cloned.1.call-update) | async-done | bytes 37748752 | tf_op jit(solution)/shard_map/all_gather | solution.py:91
  777.2 13.5 %reduce_sum.9 = f32[2,2,384,384]{3,2,1,0:T(8,128)S(1)} reduce(f32[16,2,2,384,384]{4,3,2,1,0:T(8,128)} %all-gather.8.cloned.1.call-done, f32[]{:T(128)} %constant.46.clone.1), dimensions={0}, to_apply=%region_0.2 | reduce | flops 8847360 | bytes 40108036 | tf_op jit(solution)/shard_map/reduce_sum | solution.py:91
  790.7 0.7 constant_dynamic-slice_fusion
  (13 shorter events, 0.0 us)
Async XLA Ops:
  15.1 7.6 copy-start.5
  15.1 66.8 %all-to-all-start = ((f32[384,2,1024]{2,1,0:T(2,128)}), f32[384,2,1024]{2,1,0:T(2,128)S(1)}, u32[]{:S(2)}, u32[]{:S(2)}) async-start(f32[384,2,1024]{2,1,0:T(2,128)} %reshape.66), calls=%async_computation | async-start | bytes 6291456 | tf_op jit(solution)/shard_map/all_to_all | solution.py:69
  22.6 410.8 %all-gather.6.cloned.1.call-start = ((), (), s32[]{:S(2)}) async-start(), calls=%async_computation.4 | async-start | bytes 2359296 | tf_op jit(solution)/shard_map/all_gather | solution.py:82
  102.0 1.6 copy-start.1
  152.1 7.6 copy-start.3
  187.3 5.5 copy-start.4
  198.4 10.2 %copy-start.2 = (f32[24,32,1024]{2,1,0:T(8,128)S(1)}, f32[24,32,1024]{2,1,0:T(8,128)}, u32[]{:S(2)}) copy-start(f32[24,32,1024]{2,1,0:T(8,128)} %reshape.69) | copy-start | bytes 9437188
  299.4 35.9 %copy-start = (bf16[2,24,8192]{1,2,0:T(8,128)(2,1)}, bf16[2,24,8192]{1,2,0:T(8,128)(2,1)S(1)}, u32[]{:S(2)}) copy-start(bf16[2,24,8192]{1,2,0:T(8,128)(2,1)S(1)} %pad_maximum_fusion) | copy-start | bytes 2359300
  395.0 136.3 %all-gather.4.cloned.1.call-start = ((), (), s32[]{:S(2)}) async-start(), calls=%async_computation.3 | async-start | bytes 7077888 | tf_op jit(solution)/shard_map/all_gather | solution.py:79
  433.4 343.8 %all-gather.8.cloned.1.call-start = ((), (), s32[]{:S(2)}) async-start(), calls=%async_computation.5 | async-start | bytes 40108032 | tf_op jit(solution)/shard_map/all_gather | solution.py:91
Sparse Core Ops, SparseCore 0:
  395.1 8.8 all-gather.5
  433.5 97.7 all-gather.3
  591.2 185.9 all-gather.7
